TPU v7x, 32 devices: a whole 2x2x4 slice. The times are simulated.
32 devices in a mesh: site: 2 (over y), rows: 4 (over z), cols: 2 (over core), slabs: 2 (over x).
Axes of the slice: x: 2, y: 2, z: 4, core: 2. Of those that a mesh axis runs over, the one named last changes fastest.
Arguments:
- pressure: float32 [32, 128, 64, 128], P(('site', 'rows'), 'cols', 'slabs'), parts along dimension 0, may hold values from 0.2 to 1.8
- earlier: float32 [32, 128, 64, 128], P(('site', 'rows'), 'cols', 'slabs'), parts along dimension 0, may hold values from 0.2 to 1.8
- speed_square: float32 [32, 128, 64, 128], P(('site', 'rows'), 'cols', 'slabs'), parts along dimension 0, may hold values from 0.05 to 0.3
Outputs:
- potential: float32 [32, 128, 64, 128], P(('site', 'rows'), 'cols', 'slabs'), parts along dimension 0
- pressure_end: float32 [32, 128, 64, 128], P(('site', 'rows'), 'cols', 'slabs'), parts along dimension 0
There are 2 independent parts, one for each index of `site`. A program takes and returns all parts, laid end to end along the dimension named above; each array names one. Nothing has to cross between parts.
All inputs are finite; a program needn't handle non-finite values.
Results may differ from a plain program's by a relative error of at most 0.00002.
Values sent between devices are 32-bit elements; how exact they have to be, the bound alone decides.
A program may use at most 192 MiB of HBM per device.

v0:
```python
import jax
import jax.numpy as jnp
from jax import lax
from jax.sharding import PartitionSpec as P

STEPS = 4


def extended(cells, sides, width):
    for axis, dim in sides:
        count = lax.axis_size(axis)
        head = lax.slice_in_dim(cells, 0, width, axis=dim)
        tail = lax.slice_in_dim(cells, cells.shape[dim] - width, cells.shape[dim], axis=dim)
        cells = jnp.concatenate(
            [
                lax.ppermute(tail, axis, [(i, (i + 1) % count) for i in range(count)]),
                cells,
                lax.ppermute(head, axis, [((i + 1) % count, i) for i in range(count)]),
            ],
            axis=dim,
        )
    return cells


def entering(part, axis, combine, identity):
    place = lax.axis_index(axis)
    gathered = lax.all_gather(part, axis)
    state = jnp.zeros_like(part) + jnp.asarray(identity, part.dtype)

    def one(step, state):
        return combine(state, lax.dynamic_index_in_dim(gathered, step, 0, False))

    return lax.fori_loop(0, place, one, state)


def strip_edges(values, dims):
    for dim in dims:
        values = lax.slice_in_dim(values, 1, values.shape[dim] - 1, axis=dim)
    return values


def neighbour(values, dim, start, dims):
    others = [other for other in dims if other != dim]
    values = strip_edges(values, others)
    return lax.slice_in_dim(values, start, start + values.shape[dim] - 2, axis=dim)


def one_step(padded, before, speed_square):
    middle = strip_edges(padded, (0, 1, 2))
    lower = [neighbour(padded, dim, 0, (0, 1, 2)) for dim in (0, 1, 2)]
    upper = [neighbour(padded, dim, 2, (0, 1, 2)) for dim in (0, 1, 2)]
    spread = lower[0] + upper[0] + lower[1] + upper[1] + lower[2] + upper[2] - 6.0 * middle
    return 2.0 * middle - before + speed_square * spread


def local(pressure, earlier, speed_square):
    for step in range(STEPS):
        padded = extended(pressure, (("rows", 0), ("cols", 1), ("slabs", 2)), 1)
        later = one_step(padded, earlier, speed_square)
        earlier, pressure = (pressure, later)
    here = jnp.cumsum(pressure, axis=0)
    total = lax.slice_in_dim(here, here.shape[0] - 1, here.shape[0], axis=0)

    def add_pair(earlier_total, later_total):
        return earlier_total + later_total

    below = entering(total, "rows", add_pair, jnp.zeros_like(total))
    potential = (here + below) / (pressure.shape[0] * lax.axis_size("rows"))
    return (potential, pressure)


def solution(mesh):
    placed = (
        P(("site", "rows"), "cols", "slabs", None),
        P(("site", "rows"), "cols", "slabs", None),
        P(("site", "rows"), "cols", "slabs", None),
    )
    return jax.shard_map(
        local,
        mesh=mesh,
        in_specs=placed,
        out_specs=(
            P(("site", "rows"), "cols", "slabs", None),
            P(("site", "rows"), "cols", "slabs", None),
        ),
        check_vma=False,
    )
```

profile of v0, /device:TPU:24, one launch (start us, length us, event | category | flops | bytes accessed | tf_op | source)
XLA Modules:
  0.0 395.6 jit_solution(11013965857375289950)
XLA Ops:
  7.2 1.9 fusion.36
  9.2 2.0 collective-permute-start.1
  11.2 45.3 %collective-permute-done = f32[1,64,32,128]{3,2,1,0:T(8,128)S(1)} collective-permute-done((f32[1,64,32,128]{3,2,1,0:T(8,128)S(1)}, f32[1,64,32,128]{3,2,1,0:T(8,128)S(1)}, u32[]{:S(2)}, u32[]{:S(2)}) %collective-permute-start) | collective-permute-done | bytes 1048608 | tf_op jit(solution)/shard_map/ppermute | solution.py:16
  57.3 0.5 collective-permute-start.3
  57.7 0.8 collective-permute-done.2
  59.0 1.6 collective-permute-start.4
  60.6 0.6 collective-permute-start.5
  61.2 6.2 %collective-permute-done.4 = f32[6,66,1,128]{3,1,2,0:T(8,128)S(1)} collective-permute-done((f32[6,66,1,128]{3,1,2,0:T(8,128)S(1)}, f32[6,66,1,128]{3,1,2,0:T(8,128)S(1)}, u32[]{:S(2)}, u32[]{:S(2)}) %collective-permute-start.4) | collective-permute-done | bytes 202784 | tf_op jit(solution)/shard_map/ppermute | solution.py:16
  67.6 3.9 collective-permute-done.5
  71.7 14.1 %fusion.27 = f32[4,64,32,128]{3,2,1,0:T(8,128)S(1)} fusion(f32[4,64,32,128]{3,2,1,0:T(8,128)S(1)} %copy-done, f32[6,66,1,128]{3,2,1,0:T(1,128)S(1)} %copy.27, f32[6,1,32,128]{3,2,1,0:T(8,128)S(1)} %collective-permute-done.3, f32[6,64,32,128]{3,2,1,0:T(8,128)} %copy-done.3, f32[6,1,32,128]{3,2,1,0:T(8,128)S(1)} %collective-permute-done.2, ...), kind=kLoop, calls=%fused_computation.83 | loop fusion | flops 22020096 | bytes 25767936 | tf_op jit(solution)/shard_map/add | solution.py:53
  86.0 1.0 collective-permute-start.6
  87.0 1.1 collective-permute-start.7
  88.1 23.9 %collective-permute-done.6 = f32[1,64,32,128]{3,2,1,0:T(8,128)S(1)} collective-permute-done((f32[1,64,32,128]{3,2,1,0:T(8,128)S(1)}, f32[1,64,32,128]{3,2,1,0:T(8,128)S(1)}, u32[]{:S(2)}, u32[]{:S(2)}) %collective-permute-start.6) | collective-permute-done | bytes 1048608 | tf_op jit(solution)/shard_map/ppermute | solution.py:16
  112.0 21.2 %collective-permute-done.7 = f32[1,64,32,128]{3,2,1,0:T(8,128)S(1)} collective-permute-done((f32[1,64,32,128]{3,2,1,0:T(8,128)S(1)}, f32[1,64,32,128]{3,2,1,0:T(8,128)S(1)}, u32[]{:S(2)}, u32[]{:S(2)}) %collective-permute-start.7) | collective-permute-done | bytes 1048608 | tf_op jit(solution)/shard_map/ppermute | solution.py:18
  133.8 0.8 collective-permute-done.8
  135.0 1.6 collective-permute-start.10
  136.6 0.6 collective-permute-start.11
  137.2 6.2 %collective-permute-done.10 = f32[6,66,1,128]{3,1,2,0:T(8,128)S(1)} collective-permute-done((f32[6,66,1,128]{3,1,2,0:T(8,128)S(1)}, f32[6,66,1,128]{3,1,2,0:T(8,128)S(1)}, u32[]{:S(2)}, u32[]{:S(2)}) %collective-permute-start.10) | collective-permute-done | bytes 202784 | tf_op jit(solution)/shard_map/ppermute | solution.py:16
  143.6 3.9 collective-permute-done.11
  147.8 7.2 %fusion.19 = f32[4,64,32,128]{3,2,1,0:T(8,128)S(1)} fusion(f32[4,64,32,128]{3,2,1,0:T(8,128)S(1)} %copy-done, f32[6,66,1,128]{3,2,1,0:T(1,128)S(1)} %copy.31, f32[6,1,32,128]{3,2,1,0:T(8,128)S(1)} %collective-permute-done.9, f32[6,1,32,128]{3,2,1,0:T(8,128)S(1)} %collective-permute-done.8, f32[1,64,32,128]{3,2,1,0:T(8,128)S(1)} %collective-permute-done.7, ...), kind=kLoop, calls=%fused_computation.57 | loop fusion | flops 30408704 | bytes 19476480 | tf_op jit(solution)/shard_map/add | solution.py:53
  155.1 1.8 collective-permute-start.12
  157.2 23.3 %collective-permute-done.12 = f32[1,64,32,128]{3,2,1,0:T(8,128)S(1)} collective-permute-done((f32[1,64,32,128]{3,2,1,0:T(8,128)S(1)}, f32[1,64,32,128]{3,2,1,0:T(8,128)S(1)}, u32[]{:S(2)}, u32[]{:S(2)}) %collective-permute-start.12) | collective-permute-done | bytes 1048608 | tf_op jit(solution)/shard_map/ppermute | solution.py:16
  180.4 22.7 %collective-permute-done.13 = f32[1,64,32,128]{3,2,1,0:T(8,128)S(1)} collective-permute-done((f32[1,64,32,128]{3,2,1,0:T(8,128)S(1)}, f32[1,64,32,128]{3,2,1,0:T(8,128)S(1)}, u32[]{:S(2)}, u32[]{:S(2)}) %collective-permute-start.13) | collective-permute-done | bytes 1048608 | tf_op jit(solution)/shard_map/ppermute | solution.py:18
  203.3 0.5 collective-permute-start.15
  203.8 0.8 collective-permute-done.14
  205.0 1.6 collective-permute-start.16
  206.6 0.6 collective-permute-start.17
  207.2 6.2 %collective-permute-done.16 = f32[6,66,1,128]{3,1,2,0:T(8,128)S(1)} collective-permute-done((f32[6,66,1,128]{3,1,2,0:T(8,128)S(1)}, f32[6,66,1,128]{3,1,2,0:T(8,128)S(1)}, u32[]{:S(2)}, u32[]{:S(2)}) %collective-permute-start.16) | collective-permute-done | bytes 202784 | tf_op jit(solution)/shard_map/ppermute | solution.py:16
  213.6 3.9 collective-permute-done.17
  217.7 7.1 %fusion.11 = f32[4,64,32,128]{3,2,1,0:T(8,128)S(1)} fusion(f32[4,64,32,128]{3,2,1,0:T(8,128)S(1)} %copy-done, f32[6,66,1,128]{3,2,1,0:T(1,128)S(1)} %copy.35, f32[6,1,32,128]{3,2,1,0:T(8,128)S(1)} %collective-permute-done.15, f32[6,1,32,128]{3,2,1,0:T(8,128)S(1)} %collective-permute-done.14, f32[1,64,32,128]{3,2,1,0:T(8,128)S(1)} %collective-permute-done.13, ...), kind=kLoop, calls=%fused_computation.31 | loop fusion | flops 30408704 | bytes 19476480 | tf_op jit(solution)/shard_map/add | solution.py:53
  225.0 1.8 collective-permute-start.18
  227.1 23.4 %collective-permute-done.18 = f32[1,64,32,128]{3,2,1,0:T(8,128)S(1)} collective-permute-done((f32[1,64,32,128]{3,2,1,0:T(8,128)S(1)}, f32[1,64,32,128]{3,2,1,0:T(8,128)S(1)}, u32[]{:S(2)}, u32[]{:S(2)}) %collective-permute-start.18) | collective-permute-done | bytes 1048608 | tf_op jit(solution)/shard_map/ppermute | solution.py:16
  250.6 22.1 %collective-permute-done.19 = f32[1,64,32,128]{3,2,1,0:T(8,128)S(1)} collective-permute-done((f32[1,64,32,128]{3,2,1,0:T(8,128)S(1)}, f32[1,64,32,128]{3,2,1,0:T(8,128)S(1)}, u32[]{:S(2)}, u32[]{:S(2)}) %collective-permute-start.19) | collective-permute-done | bytes 1048608 | tf_op jit(solution)/shard_map/ppermute | solution.py:18
  272.8 0.5 collective-permute-start.21
  273.3 0.8 collective-permute-done.20
  274.5 1.6 collective-permute-start.22
  276.1 0.6 collective-permute-start.23
  276.7 6.2 %collective-permute-done.22 = f32[6,66,1,128]{3,1,2,0:T(8,128)S(1)} collective-permute-done((f32[6,66,1,128]{3,1,2,0:T(8,128)S(1)}, f32[6,66,1,128]{3,1,2,0:T(8,128)S(1)}, u32[]{:S(2)}, u32[]{:S(2)}) %collective-permute-start.22) | collective-permute-done | bytes 202784 | tf_op jit(solution)/shard_map/ppermute | solution.py:16
  283.1 3.9 collective-permute-done.23
  287.3 7.1 %fusion.3 = f32[4,64,32,128]{3,2,1,0:T(8,128)S(1)} fusion(f32[4,64,32,128]{3,2,1,0:T(8,128)S(1)} %copy-done, f32[6,66,1,128]{3,2,1,0:T(1,128)S(1)} %copy.39, f32[6,1,32,128]{3,2,1,0:T(8,128)S(1)} %collective-permute-done.21, f32[6,1,32,128]{3,2,1,0:T(8,128)S(1)} %collective-permute-done.20, f32[1,64,32,128]{3,2,1,0:T(8,128)S(1)} %collective-permute-done.19, ...), kind=kLoop, calls=%fused_computation.5 | loop fusion | flops 30408704 | bytes 19476480 | tf_op jit(solution)/shard_map/add | solution.py:53
  294.4 2.9 fusion.37
  297.7 2.3 slice.360
  300.0 79.1 %all-gather.3.cloned.1.call-done = f32[4,64,32,128]{3,2,1,0:T(8,128)} async-done(((f32[1,64,32,128]{3,2,1,0:T(8,128)}), f32[4,64,32,128]{3,2,1,0:T(8,128)}) %all-gather.3.cloned.1.call-update) | async-done | bytes 4194320 | tf_op jit(solution)/shard_map/all_gather | solution.py:27
  379.3 4.6 %while.10 = (s32[]{:T(128)}, f32[1,64,32,128]{3,2,1,0:T(8,128)S(1)}, s32[]{:T(128)}, f32[4,1,64,32,128]{4,3,2,1,0:T(8,128)}, s32[]{:T(128)}, /*index=5*/s32[]{:T(128)}, s32[]{:T(128)}) while((s32[]{:T(128)}, f32[1,64,32,128]{3,2,1,0:T(8,128)S(1)}, s32[]{:T(128)}, f32[4,1,64,32,128]{4,3,2,1,0:T(8,128)}, s32[]{:T(128)}, /*index=5*/s32[]{:T(128)}, ...), condition=%wide.region_2.3_spmd, body=%wide.region_1.2_spmd.sunk | while | flops 262149 | bytes 3145843 | solution.py:33
  379.3 1.5 bitcast_add_fusion.2
  380.8 1.5 bitcast_add_fusion.2
  382.4 1.5 bitcast_add_fusion.2
  383.9 4.9 %add_multiply_fusion = f32[4,64,32,128]{3,2,1,0:T(8,128)} fusion(f32[4,64,32,128]{3,2,1,0:T(8,128)} %fusion.37, f32[64,32,128]{2,1,0:T(8,128)S(1)} %bitcast.9), kind=kLoop, calls=%fused_computation.97 | loop fusion | flops 2097152 | bytes 9437184 | tf_op jit(solution)/shard_map/div | solution.py:68
  (56 shorter events, 6.7 us)
Async XLA Ops:
  7.2 372.0 %all-gather.3.cloned.1.call-start = ((), (), s32[]{:S(2)}) async-start(), calls=%async_computation | async-start | bytes 5242880 | tf_op jit(solution)/shard_map/all_gather | solution.py:27
  7.2 49.4 %copy-start.1 = (f32[4,64,32,128]{3,2,1,0:T(8,128)S(1)}, f32[4,64,32,128]{3,2,1,0:T(8,128)}, u32[]{:S(2)}) copy-start(f32[4,64,32,128]{3,2,1,0:T(8,128)} %param.5) | copy-start | bytes 12582916
  9.1 47.4 %collective-permute-start = (f32[1,64,32,128]{3,2,1,0:T(8,128)S(1)}, f32[1,64,32,128]{3,2,1,0:T(8,128)S(1)}, u32[]{:S(2)}, u32[]{:S(2)}) collective-permute-start(f32[1,64,32,128]{3,2,1,0:T(8,128)S(1)} %get-tuple-element.71), channel_id=1, source_target_pairs={{0,4},{4,8},{8,12},{12,0},{1,5},{5,9},{9,13},{13,1},{2,6},{6,10},{... | collective-permute-start | bytes 3145736 | tf_op jit(solution)/shard_map/ppermute | solution.py:16
  9.2 47.9 %collective-permute-start.1 = (f32[1,64,32,128]{3,2,1,0:T(8,128)S(1)}, f32[1,64,32,128]{3,2,1,0:T(8,128)S(1)}, u32[]{:S(2)}, u32[]{:S(2)}) collective-permute-start(f32[1,64,32,128]{3,2,1,0:T(8,128)S(1)} %get-tuple-element.70), channel_id=1, source_target_pairs={{4,0},{8,4},{12,8},{0,12},{5,1},{9,5},{13,9},{1,13},{6,2},{10,6},{... | collective-permute-start | bytes 3145736 | tf_op jit(solution)/shard_map/ppermute | solution.py:18
  57.1 14.4 %copy-start.3 = (f32[6,64,32,128]{3,2,1,0:T(8,128)}, f32[6,64,32,128]{3,2,1,0:T(8,128)S(1)}, u32[]{:S(2)}) copy-start(f32[6,64,32,128]{3,2,1,0:T(8,128)S(1)} %constant_dynamic-update-slice_fusion) | copy-start | bytes 18874372
  57.2 1.4 collective-permute-start.2
  57.2 14.5 %copy-start = (f32[4,64,32,128]{3,2,1,0:T(8,128)S(1)}, f32[4,64,32,128]{3,2,1,0:T(8,128)}, u32[]{:S(2)}) copy-start(f32[4,64,32,128]{3,2,1,0:T(8,128)} %param.7) | copy-start | bytes 12582916
  57.3 1.4 collective-permute-start.3
  59.0 8.4 %collective-permute-start.4 = (f32[6,66,1,128]{3,1,2,0:T(8,128)S(1)}, f32[6,66,1,128]{3,1,2,0:T(8,128)S(1)}, u32[]{:S(2)}, u32[]{:S(2)}) collective-permute-start(f32[6,66,1,128]{3,1,2,0:T(8,128)S(1)} %copy.24), channel_id=1, source_target_pairs={{0,1},{1,0},{2,3},{3,2},{4,5},{5,4},{6,7},{7,6},{8,9},{9,8},{10,11... | collective-permute-start | bytes 608264 | tf_op jit(solution)/shard_map/ppermute | solution.py:16
  60.6 10.9 %collective-permute-start.5 = (f32[6,66,1,128]{3,1,2,0:T(8,128)S(1)}, f32[6,66,1,128]{3,1,2,0:T(8,128)S(1)}, u32[]{:S(2)}, u32[]{:S(2)}) collective-permute-start(f32[6,66,1,128]{3,1,2,0:T(8,128)S(1)} %copy.26), channel_id=1, source_target_pairs={{1,0},{0,1},{3,2},{2,3},{5,4},{4,5},{7,6},{6,7},{9,8},{8,9},{11,10... | collective-permute-start | bytes 608264 | tf_op jit(solution)/shard_map/ppermute | solution.py:18
  86.0 26.0 %collective-permute-start.6 = (f32[1,64,32,128]{3,2,1,0:T(8,128)S(1)}, f32[1,64,32,128]{3,2,1,0:T(8,128)S(1)}, u32[]{:S(2)}, u32[]{:S(2)}) collective-permute-start(f32[1,64,32,128]{3,2,1,0:T(8,128)S(1)} %get-tuple-element.68), channel_id=1, source_target_pairs={{0,4},{4,8},{8,12},{12,0},{1,5},{5,9},{9,13},{13,1},{2,6},{6,10},{... | collective-permute-start | bytes 3145736 | tf_op jit(solution)/shard_map/ppermute | solution.py:16
  87.0 46.1 %collective-permute-start.7 = (f32[1,64,32,128]{3,2,1,0:T(8,128)S(1)}, f32[1,64,32,128]{3,2,1,0:T(8,128)S(1)}, u32[]{:S(2)}, u32[]{:S(2)}) collective-permute-start(f32[1,64,32,128]{3,2,1,0:T(8,128)S(1)} %get-tuple-element.69), channel_id=1, source_target_pairs={{4,0},{8,4},{12,8},{0,12},{5,1},{9,5},{13,9},{1,13},{6,2},{10,6},{... | collective-permute-start | bytes 3145736 | tf_op jit(solution)/shard_map/ppermute | solution.py:18
  133.2 1.4 collective-permute-start.8
  133.3 14.5 %copy-start.2 = (f32[4,64,32,128]{3,2,1,0:T(8,128)S(1)}, f32[4,64,32,128]{3,2,1,0:T(8,128)}, u32[]{:S(2)}) copy-start(f32[4,64,32,128]{3,2,1,0:T(8,128)} %param.5) | copy-start | bytes 12582916
  133.3 1.4 collective-permute-start.9
  135.0 8.4 %collective-permute-start.10 = (f32[6,66,1,128]{3,1,2,0:T(8,128)S(1)}, f32[6,66,1,128]{3,1,2,0:T(8,128)S(1)}, u32[]{:S(2)}, u32[]{:S(2)}) collective-permute-start(f32[6,66,1,128]{3,1,2,0:T(8,128)S(1)} %copy.28), channel_id=1, source_target_pairs={{0,1},{1,0},{2,3},{3,2},{4,5},{5,4},{6,7},{7,6},{8,9},{9,8},{10,11... | collective-permute-start | bytes 608264 | tf_op jit(solution)/shard_map/ppermute | solution.py:16
  136.6 10.9 %collective-permute-start.11 = (f32[6,66,1,128]{3,1,2,0:T(8,128)S(1)}, f32[6,66,1,128]{3,1,2,0:T(8,128)S(1)}, u32[]{:S(2)}, u32[]{:S(2)}) collective-permute-start(f32[6,66,1,128]{3,1,2,0:T(8,128)S(1)} %copy.30), channel_id=1, source_target_pairs={{1,0},{0,1},{3,2},{2,3},{5,4},{4,5},{7,6},{6,7},{9,8},{8,9},{11,10... | collective-permute-start | bytes 608264 | tf_op jit(solution)/shard_map/ppermute | solution.py:18
  155.1 25.3 %collective-permute-start.12 = (f32[1,64,32,128]{3,2,1,0:T(8,128)S(1)}, f32[1,64,32,128]{3,2,1,0:T(8,128)S(1)}, u32[]{:S(2)}, u32[]{:S(2)}) collective-permute-start(f32[1,64,32,128]{3,2,1,0:T(8,128)S(1)} %get-tuple-element.66), channel_id=1, source_target_pairs={{0,4},{4,8},{8,12},{12,0},{1,5},{5,9},{9,13},{13,1},{2,6},{6,10},{... | collective-permute-start | bytes 3145736 | tf_op jit(solution)/shard_map/ppermute | solution.py:16
  156.9 46.3 %collective-permute-start.13 = (f32[1,64,32,128]{3,2,1,0:T(8,128)S(1)}, f32[1,64,32,128]{3,2,1,0:T(8,128)S(1)}, u32[]{:S(2)}, u32[]{:S(2)}) collective-permute-start(f32[1,64,32,128]{3,2,1,0:T(8,128)S(1)} %get-tuple-element.67), channel_id=1, source_target_pairs={{4,0},{8,4},{12,8},{0,12},{5,1},{9,5},{13,9},{1,13},{6,2},{10,6},{... | collective-permute-start | bytes 3145736 | tf_op jit(solution)/shard_map/ppermute | solution.py:18
  203.2 1.4 collective-permute-start.14
  203.3 1.4 collective-permute-start.15
  205.0 8.4 %collective-permute-start.16 = (f32[6,66,1,128]{3,1,2,0:T(8,128)S(1)}, f32[6,66,1,128]{3,1,2,0:T(8,128)S(1)}, u32[]{:S(2)}, u32[]{:S(2)}) collective-permute-start(f32[6,66,1,128]{3,1,2,0:T(8,128)S(1)} %copy.32), channel_id=1, source_target_pairs={{0,1},{1,0},{2,3},{3,2},{4,5},{5,4},{6,7},{7,6},{8,9},{9,8},{10,11... | collective-permute-start | bytes 608264 | tf_op jit(solution)/shard_map/ppermute | solution.py:16
  206.6 10.9 %collective-permute-start.17 = (f32[6,66,1,128]{3,1,2,0:T(8,128)S(1)}, f32[6,66,1,128]{3,1,2,0:T(8,128)S(1)}, u32[]{:S(2)}, u32[]{:S(2)}) collective-permute-start(f32[6,66,1,128]{3,1,2,0:T(8,128)S(1)} %copy.34), channel_id=1, source_target_pairs={{1,0},{0,1},{3,2},{2,3},{5,4},{4,5},{7,6},{6,7},{9,8},{8,9},{11,10... | collective-permute-start | bytes 608264 | tf_op jit(solution)/shard_map/ppermute | solution.py:18
  225.0 25.5 %collective-permute-start.18 = (f32[1,64,32,128]{3,2,1,0:T(8,128)S(1)}, f32[1,64,32,128]{3,2,1,0:T(8,128)S(1)}, u32[]{:S(2)}, u32[]{:S(2)}) collective-permute-start(f32[1,64,32,128]{3,2,1,0:T(8,128)S(1)} %get-tuple-element.64), channel_id=1, source_target_pairs={{0,4},{4,8},{8,12},{12,0},{1,5},{5,9},{9,13},{13,1},{2,6},{6,10},{... | collective-permute-start | bytes 3145736 | tf_op jit(solution)/shard_map/ppermute | solution.py:16
  226.8 45.9 %collective-permute-start.19 = (f32[1,64,32,128]{3,2,1,0:T(8,128)S(1)}, f32[1,64,32,128]{3,2,1,0:T(8,128)S(1)}, u32[]{:S(2)}, u32[]{:S(2)}) collective-permute-start(f32[1,64,32,128]{3,2,1,0:T(8,128)S(1)} %get-tuple-element.65), channel_id=1, source_target_pairs={{4,0},{8,4},{12,8},{0,12},{5,1},{9,5},{13,9},{1,13},{6,2},{10,6},{... | collective-permute-start | bytes 3145736 | tf_op jit(solution)/shard_map/ppermute | solution.py:18
  272.7 1.4 collective-permute-start.20
  272.8 1.4 collective-permute-start.21
  274.5 8.4 %collective-permute-start.22 = (f32[6,66,1,128]{3,1,2,0:T(8,128)S(1)}, f32[6,66,1,128]{3,1,2,0:T(8,128)S(1)}, u32[]{:S(2)}, u32[]{:S(2)}) collective-permute-start(f32[6,66,1,128]{3,1,2,0:T(8,128)S(1)} %copy.36), channel_id=1, source_target_pairs={{0,1},{1,0},{2,3},{3,2},{4,5},{5,4},{6,7},{7,6},{8,9},{9,8},{10,11... | collective-permute-start | bytes 608264 | tf_op jit(solution)/shard_map/ppermute | solution.py:16
  276.1 10.9 %collective-permute-start.23 = (f32[6,66,1,128]{3,1,2,0:T(8,128)S(1)}, f32[6,66,1,128]{3,1,2,0:T(8,128)S(1)}, u32[]{:S(2)}, u32[]{:S(2)}) collective-permute-start(f32[6,66,1,128]{3,1,2,0:T(8,128)S(1)} %copy.38), channel_id=1, source_target_pairs={{1,0},{0,1},{3,2},{2,3},{5,4},{4,5},{7,6},{6,7},{9,8},{8,9},{11,10... | collective-permute-start | bytes 608264 | tf_op jit(solution)/shard_map/ppermute | solution.py:18
  294.4 3.3 copy-start.4
Sparse Core Ops, SparseCore 0:
  300.1 78.9 all-gather.2
where the time goes:
time: 396 us
  waiting for transfers between devices  305 us (77%)
  other arithmetic  48.9 us (12%)
  starting transfers between devices  19.2 us (5%)
  between operations  14.4 us (4%)
  local copies, waits for them, and re-layouts  7.63 us (2%)
    ppermute x12, waiting for transfers between devices, extended(): lax.ppermute(tail, axis, [(i, (i + 1) % count) for i in range(count)])  144 us
    ppermute x12, waiting for transfers between devices, extended(): lax.ppermute(head, axis, [((i + 1) % count, i) for i in range(count)])  82.3 us
    all_gather x1, waiting for transfers between devices, entering(): gathered = lax.all_gather(part, axis)  79.1 us
    add x4, other arithmetic, one_step(): return 2.0 * middle - before + speed_square * spread  35.5 us
    ppermute x12, starting transfers between devices, extended(): lax.ppermute(tail, axis, [(i, (i + 1) % count) for i in range(count)])  11.2 us
    ppermute x12, starting transfers between devices, extended(): lax.ppermute(head, axis, [((i + 1) % count, i) for i in range(count)])  7.99 us
  transfers between devices with their start and end apart: 25, of which 24 were waited for; matrix products, arithmetic and copies ran while one was open for 0% of the time, Pallas kernels for 0%

commit v1 on v0

v1 whole, which is shorter than its diff:
```python
import functools

import jax
import jax.numpy as jnp
from jax import lax
from jax.experimental import pallas as pl
from jax.experimental.pallas import tpu as pltpu
from jax.sharding import PartitionSpec as P

STEPS = 4
MESH = pl.DeviceIdType.MESH
RING_AXES = ("rows", "cols", "slabs")


def kernel(
    ring, parts, total,
    p_in, e_in, c_in, pot_out, end_out,
    field, speed, side_out, side_in, below, sums,
    load_sem, z_send, z_recv, k_send, k_recv, i_send, i_recv, t_send, t_recv, out_sem,
):
    nj, ni, nk, _ = p_in.shape
    width = ni // parts
    row = lax.axis_index("rows")
    places = {axis: lax.axis_index(axis) for axis in RING_AXES}
    after = {axis: {axis: lax.rem(places[axis] + 1, ring[axis])} for axis in RING_AXES}
    before = {
        axis: {axis: lax.rem(places[axis] + ring[axis] - 1, ring[axis])} for axis in RING_AXES
    }

    def piece_of(q):
        half = q // 2
        return jnp.where(q % 2 == 0, half, parts - 1 - half)

    def rim(c):
        return pl.ds(1 + c * width, width)

    def inner(c):
        return pl.ds(c * width, width)

    def load(which, c):
        src = (p_in, e_in, c_in)[which].at[:, inner(c)]
        if which == 2:
            dst = speed.at[:, inner(c)]
        else:
            dst = field.at[1 - which, pl.ds(1, nj), rim(c)]
        return pltpu.make_async_copy(src, dst, load_sem.at[which, c])

    def remote(src, dst, send, recv, where):
        return pltpu.make_async_remote_copy(
            src_ref=src, dst_ref=dst, send_sem=send, recv_sem=recv,
            device_id=where, device_id_type=MESH,
        )

    def z_copy(t, way, c):
        src = field.at[t + 1, nj if way == 0 else 1, rim(c)]
        dst = field.at[t + 1, 0 if way == 0 else nj + 1, rim(c)]
        where = after["rows"] if way == 0 else before["rows"]
        return remote(src, dst, z_send.at[t, way, c], z_recv.at[t, way, c], where)

    def k_copy(t, way, c):
        where = after["slabs"] if way == 0 else before["slabs"]
        return remote(
            side_out.at[t, way, :, inner(c)], side_in.at[t, way, :, inner(c)],
            k_send.at[t, way, c], k_recv.at[t, way, c], where,
        )

    def i_copy(t, way):
        src = field.at[t + 1, pl.ds(1, nj), ni if way == 0 else 1]
        dst = field.at[t + 1, pl.ds(1, nj), 0 if way == 0 else ni + 1]
        where = after["cols"] if way == 0 else before["cols"]
        return remote(src, dst, i_send.at[t, way], i_recv.at[t, way], where)

    def t_copy(c):
        return remote(
            sums.at[inner(c)], below.at[inner(c)], t_send.at[c], t_recv.at[c], after["rows"]
        )

    def out_copy(which, c):
        src = field.at[STEPS + 1 if which == 0 else 0, pl.ds(1, nj), rim(c)]
        dst = (end_out, pot_out)[which].at[:, inner(c)]
        return pltpu.make_async_copy(src, dst, out_sem.at[which, c])

    def send_all(t, c):
        z_copy(t, 0, c).start()
        z_copy(t, 1, c).start()
        k_copy(t, 0, c).start()
        k_copy(t, 1, c).start()

        @pl.when(c == parts - 1)
        def _():
            i_copy(t, 0).start()

        @pl.when(c == 0)
        def _():
            i_copy(t, 1).start()

    def each(count, body):
        def wrapped(n, carry):
            body(n)
            return carry

        lax.fori_loop(0, count, wrapped, 0)

    for which in range(3):
        each(parts, lambda q: load(which, piece_of(q)).start())

    barrier = pltpu.get_barrier_semaphore()
    for axis in RING_AXES:
        for where in (after[axis], before[axis]):
            pl.semaphore_signal(barrier, inc=1, device_id=where, device_id_type=MESH)
    pl.semaphore_wait(barrier, 2 * len(RING_AXES))

    def begin(q):
        c = piece_of(q)
        load(0, c).wait()

        def sides(n):
            i = c * width + n
            for j in range(nj):
                side_out[0, 0, j, i] = field[1, j + 1, i + 1, nk - 1:nk]
                side_out[0, 1, j, i] = field[1, j + 1, i + 1, 0:1]

        each(width, sides)
        send_all(0, c)

    each(parts, begin)

    def wait_loads(q):
        load(1, piece_of(q)).wait()
        load(2, piece_of(q)).wait()

    each(parts, wait_loads)

    def advance(t, q, last):
        c = piece_of(q)
        k_copy(t, 0, c).wait_recv()
        k_copy(t, 1, c).wait_recv()

        @pl.when(c == 0)
        def _():
            i_copy(t, 0).wait_recv()

        @pl.when(c == parts - 1)
        def _():
            i_copy(t, 1).wait_recv()

        z_copy(t, 0, c).wait_recv()
        z_copy(t, 1, c).wait_recv()

        def line(n):
            i = c * width + n
            level = lax.broadcasted_iota(jnp.int32, (nk, 1), 0)
            column = [field[t + 1, j, i + 1] for j in range(nj + 2)]
            run = None
            for j in range(nj):
                middle = column[j + 1]
                under = jnp.where(level == 0, side_in[t, 0, j, i], pltpu.roll(middle, 1, 0))
                over = jnp.where(
                    level == nk - 1, side_in[t, 1, j, i], pltpu.roll(middle, nk - 1, 0)
                )
                spread = (
                    column[j] + column[j + 2] + field[t + 1, j + 1, i] + field[t + 1, j + 1, i + 2]
                    + under + over - 6.0 * middle
                )
                later = 2.0 * middle - field[t, j + 1, i + 1] + speed[j, i] * spread
                field[t + 2, j + 1, i + 1] = later
                if last:
                    run = later if run is None else run + later
                    field[0, j + 1, i + 1] = run
                else:
                    side_out[t + 1, 0, j, i] = later[nk - 1:nk]
                    side_out[t + 1, 1, j, i] = later[0:1]
            if last:
                sums[i] = run

        each(width, line)
        if last:
            @pl.when(row == 0)
            def _():
                t_copy(c).start()

            out_copy(0, c).start()
        else:
            send_all(t + 1, c)

    each(STEPS - 1, lambda t: each(parts, lambda q: advance(t, q, False)))
    each(parts, lambda q: advance(STEPS - 1, q, True))

    def finish(q):
        c = piece_of(q)

        @pl.when(row > 0)
        def _():
            t_copy(c).wait_recv()

            @pl.when(row < ring["rows"] - 1)
            def _():
                def passed(n):
                    i = c * width + n
                    sums[i] = sums[i] + below[i]

                each(width, passed)
                t_copy(c).start()

            def added(n):
                i = c * width + n
                base = below[i]
                for j in range(nj):
                    field[0, j + 1, i + 1] = (field[0, j + 1, i + 1] + base) / total

            each(width, added)

        @pl.when(row == 0)
        def _():
            def scaled(n):
                i = c * width + n
                for j in range(nj):
                    field[0, j + 1, i + 1] = field[0, j + 1, i + 1] / total

            each(width, scaled)

        out_copy(1, c).start()

    each(parts, finish)

    def drain(c):
        def steps(t):
            for way in range(2):
                z_copy(t, way, c).wait_send()
                k_copy(t, way, c).wait_send()

        each(STEPS, steps)

        @pl.when(row < ring["rows"] - 1)
        def _():
            t_copy(c).wait_send()

        out_copy(0, c).wait()
        out_copy(1, c).wait()

    each(parts, drain)

    def drain_ends(t):
        i_copy(t, 0).wait_send()
        i_copy(t, 1).wait_send()

    each(STEPS, drain_ends)


def local(pressure, earlier, speed_square):
    nj, ni, nk, nm = pressure.shape
    ring = {axis: lax.axis_size(axis) for axis in RING_AXES}
    parts = 8 if ni % 8 == 0 else 2
    total = float(nj * ring["rows"])
    anywhere = pl.BlockSpec(memory_space=pl.ANY)
    shape = jax.ShapeDtypeStruct(pressure.shape, jnp.float32)
    dma = pltpu.SemaphoreType.DMA
    return pl.pallas_call(
        functools.partial(kernel, ring, parts, total),
        out_shape=(shape, shape),
        in_specs=[anywhere] * 3,
        out_specs=(anywhere, anywhere),
        scratch_shapes=[
            pltpu.VMEM((STEPS + 2, nj + 2, ni + 2, nk, nm), jnp.float32),
            pltpu.VMEM((nj, ni, nk, nm), jnp.float32),
            pltpu.VMEM((STEPS, 2, nj, ni, 1, nm), jnp.float32),
            pltpu.VMEM((STEPS, 2, nj, ni, 1, nm), jnp.float32),
            pltpu.VMEM((ni, nk, nm), jnp.float32),
            pltpu.VMEM((ni, nk, nm), jnp.float32),
            dma((3, parts)),
            dma((STEPS, 2, parts)), dma((STEPS, 2, parts)),
            dma((STEPS, 2, parts)), dma((STEPS, 2, parts)),
            dma((STEPS, 2)), dma((STEPS, 2)),
            dma((parts,)), dma((parts,)),
            dma((2, parts)),
        ],
        compiler_params=pltpu.CompilerParams(
            collective_id=0, has_side_effects=True, vmem_limit_bytes=60 * 1024 * 1024
        ),
    )(pressure, earlier, speed_square)


def solution(mesh):
    placed = P(("site", "rows"), "cols", "slabs", None)
    return jax.shard_map(
        local, mesh=mesh, in_specs=(placed,) * 3, out_specs=(placed,) * 2, check_vma=False
    )
```

time: 396 us -> 227 us (0.57)
  waiting for transfers between devices: 305 us -> 0 us
  Pallas kernels: 0 us -> 220 us
  other arithmetic: 48.9 us -> 0 us
  starting transfers between devices: 19.2 us -> 0 us
  between operations: 14.4 us -> 0.65 us
    ppermute x24 -> x0, waiting for transfers between devices: 226 us -> none  [the longest x12 144 us: extended(): lax.ppermute(tail, axis, [(i, (i + 1) % count) for i in range(count)])]
    pallas_call x0 -> x1, Pallas kernels: none -> 220 us  [local(): pl.pallas_call(functools.partial(kernel, ring, parts, total), out_shape=(...]
    all_gather x1 -> x0, waiting for transfers between devices: 79.1 us -> none  [entering(): gathered = lax.all_gather(part, axis)]
    add x7 -> x0, other arithmetic: 40 us -> none  [the longest x4 35.5 us: one_step(): return 2.0 * middle - before + speed_square * spread]
    ppermute x24 -> x0, starting transfers between devices: 19.2 us -> none  [the longest x12 11.2 us: extended(): lax.ppermute(tail, axis, [(i, (i + 1) % count) for i in range(count)])]
    unnamed x12 -> x4, local copies, waits for them, and re-layouts: 0.95 us -> 6.84 us
    div x1 -> x0, other arithmetic: 4.86 us -> none  [local(): potential = (here + below) / (pressure.shape[0] * lax.axis_size('rows'))]
    slice x14 -> x0, local copies, waits for them, and re-layouts: 4.83 us -> none  [the longest x1 2.31 us: local(): total = lax.slice_in_dim(here, here.shape[0] - 1, here.shape[0], axis=0)]
  transfers between devices with their start and end apart: 25 -> 0, of which waited for: 24 -> 0; matrix products, arithmetic and copies ran while one was open for 0% -> 0% of each run, Pallas kernels for 0% -> 0%
where the time goes in v1:
time: 227 us
  Pallas kernels  220 us (97%)
  local copies, waits for them, and re-layouts  6.84 us (3%)
    pallas_call x1, Pallas kernels, local(): pl.pallas_call(functools.partial(kernel, ring, parts, total), out_shape=(...  220 us
    unnamed x4, local copies, waits for them, and re-layouts  6.84 us

profile of v1, /device:TPU:24, one launch (start us, length us, event | category | flops | bytes accessed | tf_op | source)
XLA Modules:
  0.0 227.3 jit_solution(2156257839144991768)
XLA Ops:
  0.6 219.8 %shard_map.50 = (f32[4,64,32,128]{3,2,1,0:T(8,128)}, f32[4,64,32,128]{3,2,1,0:T(8,128)}) custom-call(f32[4,64,32,128]{3,2,1,0:T(8,128)} %p_in.1, f32[4,64,32,128]{3,2,1,0:T(8,128)} %e_in.1, f32[4,64,32,128]{3,2,1,0:T(8,128)} %c_in.1), custom_call_target="tpu_custom_call" | custom-call | tf_op jit(solution)/shard_map/pallas_call | solution.py:258
  220.4 0.0 copy-start
  220.4 4.8 %copy.7 = f32[4,64,32,128]{3,2,1,0:T(8,128)} copy(f32[4,64,32,128]{3,2,1,0:T(8,128)} %get-tuple-element.4) | data formatting | bytes 8388608
  225.3 0.0 copy-done
  225.3 2.0 copy.8
Async XLA Ops:
  220.4 4.8 %copy-start = (f32[4,64,32,128]{3,2,1,0:T(8,128)S(1)}, f32[4,64,32,128]{3,2,1,0:T(8,128)}, u32[]{:S(2)}) copy-start(f32[4,64,32,128]{3,2,1,0:T(8,128)} %get-tuple-element.5) | copy-start | bytes 12582916

commit v2 on v1

--- a/solution.py
+++ b/solution.py
@@ -13,13 +13,15 @@
 
 
 def kernel(
-    ring, parts, total,
+    ring, parts, fine, scale,
     p_in, e_in, c_in, pot_out, end_out,
     field, speed, side_out, side_in, below, sums,
-    load_sem, z_send, z_recv, k_send, k_recv, i_send, i_recv, t_send, t_recv, out_sem,
+    load_sem, z_send, z_recv, k_send, k_recv, i_send, i_recv, t_send, t_recv,
 ):
     nj, ni, nk, _ = p_in.shape
     width = ni // parts
+    small = ni // fine
+    share = fine // parts
     row = lax.axis_index("rows")
     places = {axis: lax.axis_index(axis) for axis in RING_AXES}
     after = {axis: {axis: lax.rem(places[axis] + 1, ring[axis])} for axis in RING_AXES}
@@ -70,19 +72,23 @@
         where = after["cols"] if way == 0 else before["cols"]
         return remote(src, dst, i_send.at[t, way], i_recv.at[t, way], where)
 
-    def t_copy(c):
+    def first_copy(way, c):
+        src = p_in.at[nj - 1 if way == 0 else 0, inner(c)]
+        dst = field.at[1, 0 if way == 0 else nj + 1, rim(c)]
+        where = after["rows"] if way == 0 else before["rows"]
+        return remote(src, dst, z_send.at[0, way, c], z_recv.at[0, way, c], where)
+
+    def t_copy(f):
+        lines = pl.ds(f * small, small)
         return remote(
-            sums.at[inner(c)], below.at[inner(c)], t_send.at[c], t_recv.at[c], after["rows"]
+            sums.at[lines], below.at[lines], t_send.at[f], t_recv.at[f], after["rows"]
         )
 
-    def out_copy(which, c):
-        src = field.at[STEPS + 1 if which == 0 else 0, pl.ds(1, nj), rim(c)]
-        dst = (end_out, pot_out)[which].at[:, inner(c)]
-        return pltpu.make_async_copy(src, dst, out_sem.at[which, c])
-
-    def send_all(t, c):
+    def send_z(t, c):
         z_copy(t, 0, c).start()
         z_copy(t, 1, c).start()
+
+    def send_sides(t, c):
         k_copy(t, 0, c).start()
         k_copy(t, 1, c).start()
 
@@ -110,6 +116,12 @@
             pl.semaphore_signal(barrier, inc=1, device_id=where, device_id_type=MESH)
     pl.semaphore_wait(barrier, 2 * len(RING_AXES))
 
+    def begin_z(q):
+        first_copy(0, piece_of(q)).start()
+        first_copy(1, piece_of(q)).start()
+
+    each(parts, begin_z)
+
     def begin(q):
         c = piece_of(q)
         load(0, c).wait()
@@ -121,7 +133,7 @@
                 side_out[0, 1, j, i] = field[1, j + 1, i + 1, 0:1]
 
         each(width, sides)
-        send_all(0, c)
+        send_sides(0, c)
 
     each(parts, begin)
 
@@ -163,11 +175,12 @@
                     + under + over - 6.0 * middle
                 )
                 later = 2.0 * middle - field[t, j + 1, i + 1] + speed[j, i] * spread
-                field[t + 2, j + 1, i + 1] = later
                 if last:
+                    end_out[j, i] = later
                     run = later if run is None else run + later
-                    field[0, j + 1, i + 1] = run
+                    pot_out[j, i] = run
                 else:
+                    field[t + 2, j + 1, i + 1] = later
                     side_out[t + 1, 0, j, i] = later[nk - 1:nk]
                     side_out[t + 1, 1, j, i] = later[0:1]
             if last:
@@ -177,11 +190,10 @@
         if last:
             @pl.when(row == 0)
             def _():
-                t_copy(c).start()
-
-            out_copy(0, c).start()
+                each(share, lambda n: t_copy(c * share + n).start())
         else:
-            send_all(t + 1, c)
+            send_z(t + 1, c)
+            send_sides(t + 1, c)
 
     each(STEPS - 1, lambda t: each(parts, lambda q: advance(t, q, False)))
     each(parts, lambda q: advance(STEPS - 1, q, True))
@@ -191,35 +203,31 @@
 
         @pl.when(row > 0)
         def _():
-            t_copy(c).wait_recv()
-
-            @pl.when(row < ring["rows"] - 1)
-            def _():
-                def passed(n):
-                    i = c * width + n
-                    sums[i] = sums[i] + below[i]
-
-                each(width, passed)
-                t_copy(c).start()
-
-            def added(n):
-                i = c * width + n
-                base = below[i]
-                for j in range(nj):
-                    field[0, j + 1, i + 1] = (field[0, j + 1, i + 1] + base) / total
-
-            each(width, added)
+            def one(n):
+                f = c * share + n
+                t_copy(f).wait_recv()
+
+                @pl.when(row < ring["rows"] - 1)
+                def _():
+                    for m in range(small):
+                        sums[f * small + m] = sums[f * small + m] + below[f * small + m]
+                    t_copy(f).start()
+
+                for m in range(small):
+                    base = below[f * small + m]
+                    for j in range(nj):
+                        pot_out[j, f * small + m] = scale(pot_out[j, f * small + m] + base)
+
+            each(share, one)
 
         @pl.when(row == 0)
         def _():
             def scaled(n):
                 i = c * width + n
                 for j in range(nj):
-                    field[0, j + 1, i + 1] = field[0, j + 1, i + 1] / total
+                    pot_out[j, i] = scale(pot_out[j, i])
 
             each(width, scaled)
-
-        out_copy(1, c).start()
 
     each(parts, finish)
 
@@ -233,10 +241,7 @@
 
         @pl.when(row < ring["rows"] - 1)
         def _():
-            t_copy(c).wait_send()
-
-        out_copy(0, c).wait()
-        out_copy(1, c).wait()
+            each(share, lambda n: t_copy(c * share + n).wait_send())
 
     each(parts, drain)
 
@@ -251,17 +256,22 @@
     nj, ni, nk, nm = pressure.shape
     ring = {axis: lax.axis_size(axis) for axis in RING_AXES}
     parts = 8 if ni % 8 == 0 else 2
-    total = float(nj * ring["rows"])
+    fine = parts * 4 if ni % (parts * 4) == 0 else parts
+    cells = nj * ring["rows"]
+
+    def scale(values):
+        return values * (1.0 / cells) if cells & (cells - 1) == 0 else values / cells
+
     anywhere = pl.BlockSpec(memory_space=pl.ANY)
-    shape = jax.ShapeDtypeStruct(pressure.shape, jnp.float32)
+    shape = pltpu.VMEM(pressure.shape, jnp.float32)
     dma = pltpu.SemaphoreType.DMA
     return pl.pallas_call(
-        functools.partial(kernel, ring, parts, total),
+        functools.partial(kernel, ring, parts, fine, scale),
         out_shape=(shape, shape),
         in_specs=[anywhere] * 3,
-        out_specs=(anywhere, anywhere),
+        out_specs=(pl.BlockSpec(memory_space=pltpu.VMEM),) * 2,
         scratch_shapes=[
-            pltpu.VMEM((STEPS + 2, nj + 2, ni + 2, nk, nm), jnp.float32),
+            pltpu.VMEM((STEPS + 1, nj + 2, ni + 2, nk, nm), jnp.float32),
             pltpu.VMEM((nj, ni, nk, nm), jnp.float32),
             pltpu.VMEM((STEPS, 2, nj, ni, 1, nm), jnp.float32),
             pltpu.VMEM((STEPS, 2, nj, ni, 1, nm), jnp.float32),
@@ -271,11 +281,10 @@
             dma((STEPS, 2, parts)), dma((STEPS, 2, parts)),
             dma((STEPS, 2, parts)), dma((STEPS, 2, parts)),
             dma((STEPS, 2)), dma((STEPS, 2)),
-            dma((parts,)), dma((parts,)),
-            dma((2, parts)),
+            dma((fine,)), dma((fine,)),
         ],
         compiler_params=pltpu.CompilerParams(
-            collective_id=0, has_side_effects=True, vmem_limit_bytes=60 * 1024 * 1024
+            collective_id=0, has_side_effects=True, vmem_limit_bytes=46 * 1024 * 1024
         ),
     )(pressure, earlier, speed_square)
 

time: 227 us -> 220 us (0.969)
  Pallas kernels: 220 us -> 216 us
  local copies, waits for them, and re-layouts: 6.84 us -> 4.03 us
    pallas_call x1, Pallas kernels: 220 us -> 216 us  [local(): pl.pallas_call(functools.partial(kernel, ring, parts, fine, scale), out_s...]
    unnamed x4 -> x2, local copies, waits for them, and re-layouts: 6.84 us -> 4.03 us
where the time goes in v2:
time: 220 us
  Pallas kernels  216 us (98%)
  local copies, waits for them, and re-layouts  4.03 us (2%)
    pallas_call x1, Pallas kernels, local(): pl.pallas_call(functools.partial(kernel, ring, parts, fine, scale), out_s...  216 us

profile of v2, /device:TPU:24, one launch (start us, length us, event | category | flops | bytes accessed | tf_op | source)
XLA Modules:
  0.0 220.3 jit_solution(8271278042481391772)
XLA Ops:
  0.6 215.7 %shard_map.50 = (f32[4,64,32,128]{3,2,1,0:T(8,128)S(1)}, f32[4,64,32,128]{3,2,1,0:T(8,128)S(1)}) custom-call(f32[4,64,32,128]{3,2,1,0:T(8,128)} %p_in.1, f32[4,64,32,128]{3,2,1,0:T(8,128)} %e_in.1, f32[4,64,32,128]{3,2,1,0:T(8,128)} %c_in.1), custom_call_target="tpu_custom_call" | custom-call | tf_op jit(solution)/shard_map/pallas_call | solution.py:268
  216.3 2.0 copy.7
  218.3 2.0 copy.8

commit v3 on v2

--- a/solution.py
+++ b/solution.py
@@ -13,15 +13,13 @@
 
 
 def kernel(
-    ring, parts, fine, scale,
+    ring, parts, small, scale,
     p_in, e_in, c_in, pot_out, end_out,
     field, speed, side_out, side_in, below, sums,
     load_sem, z_send, z_recv, k_send, k_recv, i_send, i_recv, t_send, t_recv,
 ):
     nj, ni, nk, _ = p_in.shape
     width = ni // parts
-    small = ni // fine
-    share = fine // parts
     row = lax.axis_index("rows")
     places = {axis: lax.axis_index(axis) for axis in RING_AXES}
     after = {axis: {axis: lax.rem(places[axis] + 1, ring[axis])} for axis in RING_AXES}
@@ -78,11 +76,16 @@
         where = after["rows"] if way == 0 else before["rows"]
         return remote(src, dst, z_send.at[0, way, c], z_recv.at[0, way, c], where)
 
-    def t_copy(f):
-        lines = pl.ds(f * small, small)
+    def t_copy(first, size):
+        lines = pl.ds(first, size)
+        slot = first // small
         return remote(
-            sums.at[lines], below.at[lines], t_send.at[f], t_recv.at[f], after["rows"]
+            sums.at[lines], below.at[lines], t_send.at[slot], t_recv.at[slot], after["rows"]
         )
+
+    def totals_of(q, body):
+        start = piece_of(q) * width
+        each(width // small, lambda n: body(start + n * small, small))
 
     def send_z(t, c):
         z_copy(t, 0, c).start()
@@ -190,7 +193,7 @@
         if last:
             @pl.when(row == 0)
             def _():
-                each(share, lambda n: t_copy(c * share + n).start())
+                totals_of(q, lambda first, size: t_copy(first, size).start())
         else:
             send_z(t + 1, c)
             send_sides(t + 1, c)
@@ -201,24 +204,28 @@
     def finish(q):
         c = piece_of(q)
 
+        def one(first, size):
+            t_copy(first, size).wait_recv()
+
+            @pl.when(row < ring["rows"] - 1)
+            def _():
+                def passed(m):
+                    sums[first + m] = sums[first + m] + below[first + m]
+
+                each(size, passed)
+                t_copy(first, size).start()
+
+            def added(m):
+                i = first + m
+                base = below[i]
+                for j in range(nj):
+                    pot_out[j, i] = scale(pot_out[j, i] + base)
+
+            each(size, added)
+
         @pl.when(row > 0)
         def _():
-            def one(n):
-                f = c * share + n
-                t_copy(f).wait_recv()
-
-                @pl.when(row < ring["rows"] - 1)
-                def _():
-                    for m in range(small):
-                        sums[f * small + m] = sums[f * small + m] + below[f * small + m]
-                    t_copy(f).start()
-
-                for m in range(small):
-                    base = below[f * small + m]
-                    for j in range(nj):
-                        pot_out[j, f * small + m] = scale(pot_out[j, f * small + m] + base)
-
-            each(share, one)
+            totals_of(q, one)
 
         @pl.when(row == 0)
         def _():
@@ -231,7 +238,9 @@
 
     each(parts, finish)
 
-    def drain(c):
+    def drain(q):
+        c = piece_of(q)
+
         def steps(t):
             for way in range(2):
                 z_copy(t, way, c).wait_send()
@@ -241,7 +250,7 @@
 
         @pl.when(row < ring["rows"] - 1)
         def _():
-            each(share, lambda n: t_copy(c * share + n).wait_send())
+            totals_of(q, lambda first, size: t_copy(first, size).wait_send())
 
     each(parts, drain)
 
@@ -255,8 +264,8 @@
 def local(pressure, earlier, speed_square):
     nj, ni, nk, nm = pressure.shape
     ring = {axis: lax.axis_size(axis) for axis in RING_AXES}
-    parts = 8 if ni % 8 == 0 else 2
-    fine = parts * 4 if ni % (parts * 4) == 0 else parts
+    parts = 2
+    small = 2 if ni % (2 * parts) == 0 else 1
     cells = nj * ring["rows"]
 
     def scale(values):
@@ -266,7 +275,7 @@
     shape = pltpu.VMEM(pressure.shape, jnp.float32)
     dma = pltpu.SemaphoreType.DMA
     return pl.pallas_call(
-        functools.partial(kernel, ring, parts, fine, scale),
+        functools.partial(kernel, ring, parts, small, scale),
         out_shape=(shape, shape),
         in_specs=[anywhere] * 3,
         out_specs=(pl.BlockSpec(memory_space=pltpu.VMEM),) * 2,
@@ -281,7 +290,7 @@
             dma((STEPS, 2, parts)), dma((STEPS, 2, parts)),
             dma((STEPS, 2, parts)), dma((STEPS, 2, parts)),
             dma((STEPS, 2)), dma((STEPS, 2)),
-            dma((fine,)), dma((fine,)),
+            dma((ni // small,)), dma((ni // small,)),
         ],
         compiler_params=pltpu.CompilerParams(
             collective_id=0, has_side_effects=True, vmem_limit_bytes=46 * 1024 * 1024

time: 220 us -> 218 us (level)
  no operation moved by 1% of the time
where the time goes in v3:
time: 218 us
  Pallas kernels  214 us (98%)
  local copies, waits for them, and re-layouts  4.03 us (2%)
    pallas_call x1, Pallas kernels, local(): pl.pallas_call(functools.partial(kernel, ring, parts, small, scale), out_...  214 us

profile of v3, /device:TPU:24, one launch (start us, length us, event | category | flops | bytes accessed | tf_op | source)
XLA Modules:
  0.0 218.2 jit_solution(16675790440906587732)
XLA Ops:
  0.6 213.6 %shard_map.50 = (f32[4,64,32,128]{3,2,1,0:T(8,128)S(1)}, f32[4,64,32,128]{3,2,1,0:T(8,128)S(1)}) custom-call(f32[4,64,32,128]{3,2,1,0:T(8,128)} %p_in.1, f32[4,64,32,128]{3,2,1,0:T(8,128)} %e_in.1, f32[4,64,32,128]{3,2,1,0:T(8,128)} %c_in.1), custom_call_target="tpu_custom_call" | custom-call | tf_op jit(solution)/shard_map/pallas_call | solution.py:277
  214.2 2.0 copy.7
  216.2 2.0 copy.8
